TPU v7x, 32 devices: a whole 2x2x4 slice. The times are simulated.
32 devices in a mesh: fov: 8 (over z, x), row: 4 (over y, core).
Axes of the slice: x: 2, y: 2, z: 4, core: 2. Of those that a mesh axis runs over, the one named last changes fastest.
Arguments:
- frames: bfloat16 [8, 5, 512, 512], P('fov', None, 'row'), parts along dimension 0, may hold values from 0.01 to 13, as said below
- phase_offset: float32 [8], P('fov'), parts along dimension 0, may hold values from -3.140625 to 3.140625
- order_gain: float32 [8, 5], P('fov'), parts along dimension 0, may hold values from 0.5 to 2
- band_shift: int32 [8, 2], P('fov'), parts along dimension 0, may hold values from -96 to 96
Outputs:
- picture: float32 [8192, 1024], P(('fov', 'row')), parts along dimension 0
There are 8 independent parts, one for each index of `fov`. A program takes and returns all parts, laid end to end along the dimension named above; each array names one. Nothing has to cross between parts.
Inputs may be any that keep to these rules, and one draw needn't show every extreme that they name: `frames`: positive intensities. `band_shift`: offsets in frequency bins of the 1024-point grid, row component first.
All inputs are finite; a program needn't handle non-finite values.
Results may differ from a plain program's by a relative error of at most 0.0003.
Values sent between devices are 32-bit elements; how exact they have to be, the bound alone decides.
A program may use at most 128 MiB of HBM per device.

v0:
```python
import functools
import math

import jax
import jax.numpy as jnp
import numpy as np
from jax import lax
from jax.experimental import pallas as pl
from jax.experimental.pallas import tpu as pltpu
from jax.sharding import PartitionSpec as P

MESH = pl.DeviceIdType.MESH
wiener = 0.1
gain_out = 8.0
cut_share = 0.45
CORES = 2


def split_table(table):
    high = table.astype(np.float32).astype(jnp.bfloat16)
    low = (table - high.astype(np.float64)).astype(np.float32).astype(jnp.bfloat16)
    return np.stack([high, low])


def cos_sin(points, freqs, length):
    angle = 2.0 * math.pi * ((points[:, None] * freqs[None, :]) % length) / length
    return np.cos(angle), np.sin(angle)


def tables(pixels, count):
    half = pixels // 2
    share = half // count
    chips = count // CORES
    points = np.arange(pixels)
    freqs = np.arange(half)
    alternate = 1.0 - 2.0 * (points % 2)
    cos_f, sin_f = cos_sin(points, freqs, pixels)
    sin_f[:, 0] = alternate

    def by_device(cos_part, sin_part):
        rows = cos_part.shape[0]
        both = np.stack([cos_part.reshape(rows, count, share), sin_part.reshape(rows, count, share)], axis=2)
        return both.reshape(rows, count * 2 * share)

    width = CORES * 2 * share
    lead = by_device(cos_f, sin_f).reshape(pixels, chips, width).transpose(1, 0, 2)
    column = np.concatenate([cos_f, sin_f], axis=1).T
    column = column.reshape(pixels, chips, pixels // chips).transpose(1, 0, 2)
    inverse = []
    for odd in range(2):
        cos_i, sin_i = cos_sin(2 * points + odd, freqs, 2 * pixels)
        sin_i[:, 0] = alternate
        inverse.append(np.concatenate([cos_i, sin_i], axis=1))
    inverse = np.stack(inverse)
    wide = np.arange(2 * pixels)
    cos_w, sin_w = cos_sin(wide, freqs, 2 * pixels)
    sin_w[:, 0] = 1.0 - 2.0 * ((wide // 2) % 2)
    last = by_device(cos_w, sin_w).T.reshape(chips, width, 2 * pixels)
    return tuple(split_table(t) for t in (lead, column, inverse, last))


def otf_polynomial():
    nodes = 0.5 + 0.5 * np.cos(math.pi * (np.arange(64) + 0.5) / 64)
    nodes = np.minimum(nodes, 0.9985)
    root = np.sqrt(1 - nodes * nodes)
    values = 2 / math.pi * (np.arccos(nodes) - nodes * root) / root**3
    fit = np.polynomial.chebyshev.Chebyshev.fit(nodes, values, 10, domain=[0, 1])
    poly = fit.convert(kind=np.polynomial.Polynomial).coef
    return [float(c) for c in poly[::-1]]


def halves(value):
    high = value.astype(jnp.bfloat16)
    return high, (value - high.astype(jnp.float32)).astype(jnp.bfloat16)


def dot(left, right):
    return jnp.dot(left, right, preferred_element_type=jnp.float32)


def dot3(left_hi, left_lo, right_hi, right_lo):
    return dot(left_hi, right_hi) + (dot(left_hi, right_lo) + dot(left_lo, right_hi))


def kernel(count, poly, frames, offset, gain, shift, lead_h, column_h, inverse_h, last_h, out,
           lead, column, inverse, last, tot_send, tot, planes, send1, recv1, mixed, weights, coef,
           send2, recv2, woven, table_sem, tot_ss, tot_rs, ss1, rs1, ss2, rs2):
    me = lax.axis_index("row")
    chips = count // CORES
    chip, core = me // CORES, me % CORES
    phases, rows, pixels = frames.shape[1:]
    half = pixels // 2
    share = half // count
    lanes = 2 * share
    others = [lax.rem(me + step, count) for step in range(1, count)]
    far_chips = [lax.rem(chip + step, chips) for step in range(1, chips)]
    sibling = chip * CORES + 1 - core
    far = [(c, c * CORES + k) for c in far_chips for k in range(CORES)]

    loads = []
    for idx, (source, target) in enumerate(
        ((lead_h, lead), (column_h, column), (inverse_h, inverse), (last_h, last))
    ):
        loads.append(pltpu.make_async_copy(source, target, table_sem.at[idx]))
    loads[0].start()

    lane8 = lax.broadcasted_iota(jnp.int32, (8, 128), 1)
    part = jnp.zeros((8, 128), jnp.float32)
    for p in range(phases):
        f = frames[0, p].astype(jnp.float32)
        s = jnp.sum(jnp.sum(f, axis=0, keepdims=True), axis=1, keepdims=True)
        part = part + jnp.where(lane8 == p, s, 0.0)
    tot_send[...] = part
    tot[me] = part

    barrier = pltpu.get_barrier_semaphore()
    for peer in others:
        pl.semaphore_signal(barrier, inc=1, device_id={"row": peer}, device_id_type=MESH)
    pl.semaphore_wait(barrier, count - 1)

    def tot_copy(peer, slot):
        return pltpu.make_async_remote_copy(
            src_ref=tot_send, dst_ref=tot.at[slot], send_sem=tot_ss.at[peer], recv_sem=tot_rs.at[slot],
            device_id={"row": peer}, device_id_type=MESH)

    for peer in others:
        tot_copy(peer, me).start()
    for load in loads[1:]:
        load.start()

    shift_y, shift_x = shift[0, 0], shift[0, 1]
    inv_cut = 1.0 / (cut_share * pixels)
    scale_out = gain_out / (4.0 * pixels * pixels)

    def wrap(value):
        return ((value + half) & (pixels - 1)) - half

    def lane_freq(shape):
        lane = lax.broadcasted_iota(jnp.int32, shape, 1)
        base = me * share
        plus = base + lane
        minus = base + lane - share
        minus = jnp.where(minus == 0, -half, minus)
        return jnp.where(lane < share, plus, -minus)

    def row_freq(first, sign, shape):
        row = first + lax.broadcasted_iota(jnp.int32, shape, 0)
        if sign == 0:
            return row
        return jnp.where(row == 0, half, -row)

    def placed(freq, order, shift_val):
        return order * shift_val + wrap(freq - order * shift_val)

    def curve(sq_y, sq_x):
        t = jnp.minimum(sq_y + sq_x, 1.0)
        r = t * lax.rsqrt(jnp.maximum(t, 1e-30))
        u = 1.0 - t
        v = u * lax.rsqrt(jnp.maximum(u, 1e-30))
        acc = jnp.full(t.shape, poly[0], jnp.float32)
        for c in poly[1:]:
            acc = acc * r + c
        return acc * (u * v)

    step = 16
    orders = phases // 2 + 1
    mid = phases // 2
    gains = [gain[0, j] for j in range(phases)]

    def make_weights(order):
        big_x = placed(lane_freq((step, lanes)), order, shift_x)
        sq_xs = []
        for j in range(phases):
            fx = (big_x - (j - mid) * shift_x).astype(jnp.float32) * inv_cut
            sq_xs.append(fx * fx)

        def body(i, carry):
            first = pl.multiple_of(i * step, step)
            for sign in range(2):
                big_y = placed(row_freq(first, sign, (step, lanes)), order, shift_y)
                den = jnp.full((step, lanes), wiener, jnp.float32)
                den_m = jnp.full((step, lanes), wiener, jnp.float32)
                own = None
                for j in range(phases):
                    fy = (big_y - (j - mid) * shift_y).astype(jnp.float32) * inv_cut
                    value = curve(fy * fy, sq_xs[j])
                    sq = value * value
                    den = den + (gains[j] * gains[j]) * sq
                    den_m = den_m + (gains[phases - 1 - j] * gains[phases - 1 - j]) * sq
                    if j == mid + order:
                        own = value
                if order == 0:
                    w = own * (gains[mid] * scale_out) / den
                else:
                    w = own * scale_out * (gains[mid + order] / den + gains[mid - order] / den_m)
                weights[order, sign, pl.ds(first, step), :] = w
            return carry

        lax.fori_loop(0, half // step, body, 0)

    make_weights(0)

    for peer in others:
        tot_copy(peer, peer).wait_recv()
    total = tot[0]
    for d in range(1, count):
        total = total + tot[d]
    level = jnp.where(lane8 < phases, float(pixels * pixels), 0.0) / jnp.where(lane8 < phases, total, 1.0)
    level = level / phases
    angle = 2.0 * math.pi / phases * lane8.astype(jnp.float32) + offset[0]

    col = lax.broadcasted_iota(jnp.int32, (8, pixels), 1)
    row = lax.broadcasted_iota(jnp.int32, (rows, 128), 0) + me * rows
    turn = 2.0 * math.pi / pixels

    groups = [(0, 2), (2, 2), (4, 1)]

    def send1_copy(dest, slot_chip, slot_core, source, g):
        first, wide = groups[g]
        window = pl.ds(first * lanes, wide * lanes)
        return pltpu.make_async_remote_copy(
            src_ref=send1.at[dest, :, window],
            dst_ref=recv1.at[slot_chip, pl.ds(pl.multiple_of(slot_core * rows, rows), rows), window],
            send_sem=ss1.at[dest, g], recv_sem=rs1.at[source, g],
            device_id={"row": dest}, device_id_type=MESH)

    loads[0].wait()
    for g, (first, wide) in enumerate(groups):
        order = 0 if wide == 1 else g + 1
        coef_re = level * jnp.cos(order * angle)
        if order == 0:
            band = coef_re[:1, 0:1] * frames[0, 0].astype(jnp.float32)
            for p in range(1, phases):
                band = band + coef_re[:1, p:p + 1] * frames[0, p].astype(jnp.float32)
            parts = [band]
        else:
            coef_im = -level * jnp.sin(order * angle)
            band_re = coef_re[:1, 0:1] * frames[0, 0].astype(jnp.float32)
            band_im = coef_im[:1, 0:1] * frames[0, 0].astype(jnp.float32)
            for p in range(1, phases):
                f = frames[0, p].astype(jnp.float32)
                band_re = band_re + coef_re[:1, p:p + 1] * f
                band_im = band_im + coef_im[:1, p:p + 1] * f
            arg_x = ((col * (order * shift_x)) & (pixels - 1)).astype(jnp.float32) * turn
            arg_y = ((row * (order * shift_y)) & (pixels - 1)).astype(jnp.float32) * turn
            cx, sx = jnp.cos(arg_x)[:1], jnp.sin(arg_x)[:1]
            cy, sy = jnp.cos(arg_y)[:, :1], jnp.sin(arg_y)[:, :1]
            ph_re = cy * cx - sy * sx
            ph_im = cy * sx + sy * cx
            parts = [band_re * ph_re - band_im * ph_im, band_re * ph_im + band_im * ph_re]
        for k, value in enumerate(parts):
            hi, lo = halves(value)
            planes[0, pl.ds((first + k) * rows, rows), :] = hi
            planes[1, pl.ds((first + k) * rows, rows), :] = lo
        span = pl.ds(first * rows, wide * rows)
        for c in far_chips:
            result = dot3(planes[0, span, :], planes[1, span, :], lead[0, c], lead[1, c])
            for k in range(wide):
                for kc in range(CORES):
                    send1[c * CORES + kc, :, pl.ds((first + k) * lanes, lanes)] = result[
                        k * rows:(k + 1) * rows, kc * lanes:(kc + 1) * lanes]
            for kc in range(CORES):
                send1_copy(c * CORES + kc, chip, core, me, g).start()
    mine = pl.ds(pl.multiple_of(core * rows, rows), rows)
    for g, (first, wide) in enumerate(groups):
        span = pl.ds(first * rows, wide * rows)
        result = dot3(planes[0, span, :], planes[1, span, :], lead[0, chip], lead[1, chip])
        for k in range(wide):
            block = result[k * rows:(k + 1) * rows]
            low_half, high_half = block[:, :lanes], block[:, lanes:]
            window = pl.ds((first + k) * lanes, lanes)
            recv1[chip, mine, window] = jnp.where(core == 0, low_half, high_half)
            send1[sibling, :, window] = jnp.where(core == 0, high_half, low_half)
        send1_copy(sibling, chip, core, me, g).start()

    for order in range(1, orders):
        make_weights(order)

    loads[1].wait()
    for g, (first, wide) in enumerate(groups):
        window = pl.ds(first * lanes, wide * lanes)
        send1_copy(sibling, chip, 1 - core, sibling, g).wait_recv()
        hi, lo = halves(recv1[chip, :, window])
        mixed[:, window] = dot3(column[0, chip], column[1, chip], hi, lo)
    for c in far_chips:
        for g, (first, wide) in enumerate(groups):
            window = pl.ds(first * lanes, wide * lanes)
            for kc in range(CORES):
                send1_copy(c * CORES + kc, c, kc, c * CORES + kc, g).wait_recv()
            hi, lo = halves(recv1[c, :, window])
            mixed[:, window] += dot3(column[0, c], column[1, c], hi, lo)

    lane = lax.broadcasted_iota(jnp.int32, (step, lanes), 1)
    low_lanes = lane < share
    special = jnp.logical_and(me == 0, jnp.logical_or(lane == 0, lane == share))
    special_top = jnp.logical_and(special, lane == share)
    freq_x = lane_freq((step, lanes))
    sign_x = jnp.where(low_lanes, 1.0, -1.0)
    parity_x = []
    for order in range(orders):
        turns = (placed(freq_x, order, shift_x) - freq_x) // pixels
        parity_x.append((1 - 2 * (turns & 1)).astype(jnp.float32))

    def turn_lanes(value):
        return pltpu.roll(value, share, 1)

    def combine(i, carry):
        first = pl.multiple_of(i * step, step)
        row0 = (first + lax.broadcasted_iota(jnp.int32, (step, lanes), 0)) == 0
        spectra = []
        for plane in range(phases):
            window = pl.ds(plane * lanes, lanes)
            upper = mixed[pl.ds(first, step), window]
            lower = mixed[pl.ds(half + first, step), window]
            upper_t, lower_t = turn_lanes(upper), turn_lanes(lower)
            as_is = jnp.logical_or(low_lanes, special)
            cc = jnp.where(as_is, upper, upper_t)
            sc = jnp.where(as_is, lower, lower_t)
            cs = jnp.where(special, 0.0, jnp.where(low_lanes, upper_t, upper)) * sign_x
            ss = jnp.where(special, 0.0, jnp.where(low_lanes, lower_t, lower)) * sign_x
            plus = (jnp.where(row0, cc, cc - ss), -jnp.where(row0, cs, sc + cs))
            minus = (jnp.where(row0, sc, cc + ss), jnp.where(row0, -ss, sc - cs))
            spectra.append((plus, minus))
        terms = []
        for sign in range(2):
            freq_y = row_freq(first, sign, (step, lanes))
            for order in range(orders):
                if order == 0:
                    re, im = spectra[phases - 1][sign]
                else:
                    rr, ri = spectra[2 * order - 2][sign]
                    ir, ii = spectra[2 * order - 1][sign]
                    re, im = rr - ii, ri + ir
                w = weights[order, sign, pl.ds(first, step), :]
                turns = (placed(freq_y, order, shift_y) - freq_y) // pixels
                terms.append((re * w, im * w, (1 - 2 * (turns & 1)).astype(jnp.float32)))
        for a in range(2):
            for b in range(2):
                sums = []
                for sign in range(2):
                    tot_re, tot_im = None, None
                    for order in range(orders):
                        re, im, par_y = terms[sign * orders + order]
                        factor = None
                        if a:
                            factor = par_y
                        if b:
                            factor = parity_x[order] if factor is None else factor * parity_x[order]
                        if factor is not None:
                            re, im = re * factor, im * factor
                        tot_re = re if tot_re is None else tot_re + re
                        tot_im = im if tot_im is None else tot_im + im
                    sums.append((tot_re, tot_im))
                (pr, pi), (mr, mi) = sums
                even_r = jnp.where(row0, pr, pr + mr)
                even_i = jnp.where(row0, pi, pi + mi)
                if a == 0:
                    odd_r = jnp.where(row0, mi, pr - mr)
                    odd_i = jnp.where(row0, -mr, pi - mi)
                else:
                    odd_r = jnp.where(row0, mr, pr - mr)
                    odd_i = jnp.where(row0, mi, pi - mi)

                def fold(x, y):
                    lo_val = x + turn_lanes(x)
                    hi_val = y - turn_lanes(y)
                    res = jnp.where(low_lanes, lo_val, hi_val)
                    res = jnp.where(special, x, res)
                    if b:
                        res = jnp.where(special_top, -y, res)
                    return res

                upper = fold(even_r, even_i)
                lower = fold(-odd_i, odd_r)
                window = pl.ds(b * lanes, lanes)
                hi, lo = halves(upper)
                coef[0, a, pl.ds(first, step), window] = hi
                coef[1, a, pl.ds(first, step), window] = lo
                hi, lo = halves(lower)
                coef[0, a, pl.ds(half + first, step), window] = hi
                coef[1, a, pl.ds(half + first, step), window] = lo
        return carry

    lax.fori_loop(0, half // step, combine, 0)

    def send2_copy(dest, slot_chip, slot_core, source, a):
        block = pl.ds(a * rows, rows)
        return pltpu.make_async_remote_copy(
            src_ref=send2.at[dest, :, block, :],
            dst_ref=recv2.at[slot_chip, :, block, pl.ds(pl.multiple_of(slot_core * lanes, lanes), lanes)],
            send_sem=ss2.at[dest, a], recv_sem=rs2.at[source, a],
            device_id={"row": dest}, device_id_type=MESH)

    loads[2].wait()
    for a in range(2):
        for _, dest in far:
            t = pl.ds(pl.multiple_of(dest * rows, rows), rows)
            result = dot3(inverse[0, a, t, :], inverse[1, a, t, :], coef[0, a], coef[1, a])
            for b in range(2):
                send2[dest, b, pl.ds(a * rows, rows), :] = result[:, b * lanes:(b + 1) * lanes]
            send2_copy(dest, chip, core, me, a).start()
    slot = pl.ds(pl.multiple_of(core * lanes, lanes), lanes)
    for a in range(2):
        for dest in (sibling, me):
            t = pl.ds(pl.multiple_of(dest * rows, rows), rows)
            result = dot3(inverse[0, a, t, :], inverse[1, a, t, :], coef[0, a], coef[1, a])
            for b in range(2):
                piece = result[:, b * lanes:(b + 1) * lanes]
                if dest is me:
                    recv2[chip, b, pl.ds(a * rows, rows), slot] = piece
                else:
                    send2[dest, b, pl.ds(a * rows, rows), :] = piece
            if dest is not me:
                send2_copy(dest, chip, core, me, a).start()

    loads[3].wait()
    for a in range(2):
        send2_copy(sibling, chip, 1 - core, sibling, a).wait_recv()
    wide_step = 256
    even_lane = (lax.broadcasted_iota(jnp.int32, (rows, wide_step), 1) & 1) == 0
    for stage, c in enumerate([chip] + far_chips):
        for a in range(2):
            if stage:
                for kc in range(CORES):
                    send2_copy(c * CORES + kc, c, kc, c * CORES + kc, a).wait_recv()
            block = pl.ds(a * rows, rows)
            for x in range(0, 2 * pixels, wide_step):
                span = pl.ds(x, wide_step)
                values = []
                for b in range(2):
                    hi, lo = halves(recv2[c, b, block, :])
                    values.append(dot3(hi, lo, last[0, c, :, span], last[1, c, :, span]))
                value = jnp.where(even_lane, values[0], values[1])
                place = pl.ds(a, rows, stride=2)
                for k in range(wide_step // 128):
                    piece = value[:, k * 128:(k + 1) * 128]
                    tile = x // 128 + k
                    if stage:
                        piece = piece + woven[tile, place, :]
                    woven[tile, place, :] = piece
    for tile in range(2 * pixels // 128):
        out[:, pl.ds(tile * 128, 128)] = woven[tile]

    for peer in others:
        tot_copy(peer, me).wait_send()
        for g in range(len(groups)):
            send1_copy(peer, chip, core, me, g).wait_send()
        for a in range(2):
            send2_copy(peer, chip, core, me, a).wait_send()


def solution(mesh):
    count = mesh.shape["row"]

    def per_device(frames, phase_offset, order_gain, band_shift):
        phases, rows, pixels = frames.shape[1:]
        lanes = pixels // count
        chips = count // CORES
        lead, column, inverse, last = tables(pixels, count)
        vmem = pl.BlockSpec(memory_space=pltpu.VMEM)
        smem = pl.BlockSpec(memory_space=pltpu.SMEM)
        hbm = pl.BlockSpec(memory_space=pl.ANY)
        bf16, f32 = jnp.bfloat16, jnp.float32
        dma = pltpu.SemaphoreType.DMA
        return pl.pallas_call(
            functools.partial(kernel, count, otf_polynomial()),
            out_shape=jax.ShapeDtypeStruct((2 * rows, 2 * pixels), f32),
            in_specs=[vmem, smem, smem, smem, hbm, hbm, hbm, hbm],
            out_specs=vmem,
            scratch_shapes=[
                pltpu.VMEM(lead.shape, bf16),
                pltpu.VMEM(column.shape, bf16),
                pltpu.VMEM(inverse.shape, bf16),
                pltpu.VMEM(last.shape, bf16),
                pltpu.VMEM((8, 128), f32),
                pltpu.VMEM((count, 8, 128), f32),
                pltpu.VMEM((2, phases * rows, pixels), bf16),
                pltpu.VMEM((count, rows, phases * lanes), f32),
                pltpu.VMEM((chips, CORES * rows, phases * lanes), f32),
                pltpu.VMEM((pixels, phases * lanes), f32),
                pltpu.VMEM((phases // 2 + 1, 2, pixels // 2, lanes), f32),
                pltpu.VMEM((2, 2, pixels, 2 * lanes), bf16),
                pltpu.VMEM((count, 2, 2 * rows, lanes), f32),
                pltpu.VMEM((chips, 2, 2 * rows, CORES * lanes), f32),
                pltpu.VMEM((2 * pixels // 128, 2 * rows, 128), f32),
                dma((4,)),
                dma((count,)), dma((count,)),
                dma((count, 3)), dma((count, 3)),
                dma((count, 2)), dma((count, 2)),
            ],
            compiler_params=pltpu.CompilerParams(
                collective_id=0, has_side_effects=True, vmem_limit_bytes=60000000
            ),
        )(frames, phase_offset, order_gain, band_shift,
          jnp.asarray(lead), jnp.asarray(column), jnp.asarray(inverse), jnp.asarray(last))

    in_specs = (P("fov", None, "row", None), P("fov"), P("fov", None), P("fov", None))
    return jax.shard_map(
        per_device, mesh=mesh, in_specs=in_specs, out_specs=P(("fov", "row"), None), check_vma=False
    )
```

profile of v0, /device:TPU:1, one launch (start us, length us, event | category | flops | bytes accessed | tf_op | source)
XLA Modules:
  0.0 45.3 jit_solution(3841696976133728463)
XLA Ops:
  0.7 42.4 %shard_map.82 = f32[256,1024]{1,0:T(8,128)} custom-call(bf16[1,5,128,512]{3,2,1,0:T(8,128)(2,1)} %frames.1, f32[1]{0:T(128)S(6)} %copy.10.offset, f32[1,5]{1,0:T(1,128)} %gain.1, s32[1,2]{1,0:T(1,128)} %shift.1, bf16[2,2,512,256]{3,2,1,0:T(8,128)(2,1)} %constant.8.clone.lead_h, bf16[2,2,512,256]{3,2,1,0:T(8,128)(2,1)} %constant.9.clone.column_h, ...), custom_call_target="tpu_custom_call" | custom-call | tf_op jit(solution)/shard_map/pallas_call | solution.py:465
  43.0 2.3 %copy.11 = f32[256,1024]{1,0:T(8,128)} copy(f32[256,1024]{1,0:T(8,128)} %shard_map.82) | data formatting | bytes 2097152
where the time goes:
time: 45.5 us; the launch traced here: 45.3 us
  Pallas kernels  42.4 us (93%)
  local copies, waits for them, and re-layouts  2.31 us (5%)
  between operations  0.66 us (1%)
    pallas_call x1, Pallas kernels, per_device(): pl.pallas_call(functools.partial(kernel, count, otf_polynomial()), out_sh...  42.4 us
    unnamed x1, local copies, waits for them, and re-layouts  2.31 us

commit v1 on v0

--- a/solution.py
+++ b/solution.py
@@ -198,7 +198,16 @@
 
         lax.fori_loop(0, half // step, body, 0)
 
-    make_weights(0)
+    col = lax.broadcasted_iota(jnp.int32, (8, pixels), 1)
+    row = lax.broadcasted_iota(jnp.int32, (rows, 128), 0) + me * rows
+    turn = 2.0 * math.pi / pixels
+    waves = {}
+    for order in range(1, orders):
+        arg_x = ((col * (order * shift_x)) & (pixels - 1)).astype(jnp.float32) * turn
+        arg_y = ((row * (order * shift_y)) & (pixels - 1)).astype(jnp.float32) * turn
+        waves[order] = (jnp.cos(arg_x)[:1], jnp.sin(arg_x)[:1], jnp.cos(arg_y)[:, :1], jnp.sin(arg_y)[:, :1])
+    angle = 2.0 * math.pi / phases * lane8.astype(jnp.float32) + offset[0]
+    unmix = {order: (jnp.cos(order * angle), jnp.sin(order * angle)) for order in range(orders)}
 
     for peer in others:
         tot_copy(peer, peer).wait_recv()
@@ -207,11 +216,6 @@
         total = total + tot[d]
     level = jnp.where(lane8 < phases, float(pixels * pixels), 0.0) / jnp.where(lane8 < phases, total, 1.0)
     level = level / phases
-    angle = 2.0 * math.pi / phases * lane8.astype(jnp.float32) + offset[0]
-
-    col = lax.broadcasted_iota(jnp.int32, (8, pixels), 1)
-    row = lax.broadcasted_iota(jnp.int32, (rows, 128), 0) + me * rows
-    turn = 2.0 * math.pi / pixels
 
     groups = [(0, 2), (2, 2), (4, 1)]
 
@@ -227,24 +231,21 @@
     loads[0].wait()
     for g, (first, wide) in enumerate(groups):
         order = 0 if wide == 1 else g + 1
-        coef_re = level * jnp.cos(order * angle)
+        coef_re = level * unmix[order][0]
         if order == 0:
             band = coef_re[:1, 0:1] * frames[0, 0].astype(jnp.float32)
             for p in range(1, phases):
                 band = band + coef_re[:1, p:p + 1] * frames[0, p].astype(jnp.float32)
             parts = [band]
         else:
-            coef_im = -level * jnp.sin(order * angle)
+            coef_im = -level * unmix[order][1]
             band_re = coef_re[:1, 0:1] * frames[0, 0].astype(jnp.float32)
             band_im = coef_im[:1, 0:1] * frames[0, 0].astype(jnp.float32)
             for p in range(1, phases):
                 f = frames[0, p].astype(jnp.float32)
                 band_re = band_re + coef_re[:1, p:p + 1] * f
                 band_im = band_im + coef_im[:1, p:p + 1] * f
-            arg_x = ((col * (order * shift_x)) & (pixels - 1)).astype(jnp.float32) * turn
-            arg_y = ((row * (order * shift_y)) & (pixels - 1)).astype(jnp.float32) * turn
-            cx, sx = jnp.cos(arg_x)[:1], jnp.sin(arg_x)[:1]
-            cy, sy = jnp.cos(arg_y)[:, :1], jnp.sin(arg_y)[:, :1]
+            cx, sx, cy, sy = waves[order]
             ph_re = cy * cx - sy * sx
             ph_im = cy * sx + sy * cx
             parts = [band_re * ph_re - band_im * ph_im, band_re * ph_im + band_im * ph_re]
@@ -273,7 +274,7 @@
             send1[sibling, :, window] = jnp.where(core == 0, high_half, low_half)
         send1_copy(sibling, chip, core, me, g).start()
 
-    for order in range(1, orders):
+    for order in range(orders):
         make_weights(order)
 
     loads[1].wait()
@@ -464,7 +465,7 @@
         dma = pltpu.SemaphoreType.DMA
         return pl.pallas_call(
             functools.partial(kernel, count, otf_polynomial()),
-            out_shape=jax.ShapeDtypeStruct((2 * rows, 2 * pixels), f32),
+            out_shape=pltpu.VMEM((2 * rows, 2 * pixels), f32),
             in_specs=[vmem, smem, smem, smem, hbm, hbm, hbm, hbm],
             out_specs=vmem,
             scratch_shapes=[

time: 45.5 us -> 42.3 us (0.930)
  Pallas kernels: 42.4 us -> 40.6 us
  local copies, waits for them, and re-layouts: 2.31 us -> 0.97 us
    pallas_call x1, Pallas kernels: 42.4 us -> 40.6 us  [per_device(): pl.pallas_call(functools.partial(kernel, count, otf_polynomial()), out_sh...]
    unnamed x1, local copies, waits for them, and re-layouts: 2.31 us -> 0.97 us
where the time goes in v1:
time: 42.3 us; the launch traced here: 42.2 us
  Pallas kernels  40.6 us (96%)
  local copies, waits for them, and re-layouts  0.97 us (2%)
  between operations  0.66 us (2%)
    pallas_call x1, Pallas kernels, per_device(): pl.pallas_call(functools.partial(kernel, count, otf_polynomial()), out_sh...  40.6 us
    unnamed x1, local copies, waits for them, and re-layouts  0.97 us

profile of v1, /device:TPU:1, one launch (start us, length us, event | category | flops | bytes accessed | tf_op | source)
XLA Modules:
  0.0 42.2 jit_solution(16394480259338583060)
XLA Ops:
  0.7 40.6 %shard_map.82 = f32[256,1024]{1,0:T(8,128)S(1)} custom-call(bf16[1,5,128,512]{3,2,1,0:T(8,128)(2,1)} %frames.1, f32[1]{0:T(128)S(6)} %copy.11.offset, f32[1,5]{1,0:T(1,128)} %gain.1, s32[1,2]{1,0:T(1,128)} %shift.1, bf16[2,2,512,256]{3,2,1,0:T(8,128)(2,1)} %constant.8.clone.lead_h, bf16[2,2,512,256]{3,2,1,0:T(8,128)(2,1)} %constant.9.clone.column_h, ...), custom_call_target="tpu_custom_call" | custom-call | tf_op jit(solution)/shard_map/pallas_call | solution.py:466
  41.2 1.0 %copy.10 = f32[256,1024]{1,0:T(8,128)} copy(f32[256,1024]{1,0:T(8,128)S(1)} %shard_map.82) | data formatting | bytes 2097152
